TPU v7x, 32 devices: a whole 2x2x4 slice. The times are simulated.
32 devices in a mesh: dom: 4 (over z), grp: 8 (over y, x, core).
Axes of the slice: x: 2, y: 2, z: 4, core: 2. Of those that a mesh axis runs over, the one named last changes fastest.
Arguments:
- master_rows: bfloat16 [8, 512, 512], P('grp', 'dom'), may hold values from -6 to 6
- cotangent: bfloat16 [8, 512, 512], P('grp', 'dom'), may hold values from -6 to 6
- relation_weight: bfloat16 [4, 512, 512], replicated, may hold values from -0.125 to 0.125
- self_weight: bfloat16 [512, 512], replicated, may hold values from -0.25 to 0.25
- edge_source: int32 [8, 8192], P('grp', 'dom'), may hold values from 0 to 191
- edge_target: int32 [8, 8192], P('grp', 'dom'), may hold values from 0 to 191
- edge_relation: int32 [8, 8192], P('grp', 'dom'), may hold values from 0 to 3
- send_rows: int32 [8, 256], P('grp', 'dom'), may hold values from 0 to 127
- send_counts: int32 [8, 16], P('grp', 'dom'), may hold values from 4 to 16, as said below
Outputs:
- activation: bfloat16 [8, 512, 512], P('grp', 'dom')
- input_grad: bfloat16 [8, 512, 512], P('grp', 'dom')
- weight_grads: float32 [5, 512, 512], P(None, 'grp')
Inputs may be any that keep to these rules, and one draw needn't show every extreme that they name: `send_counts`: on every device the count for some peer is exactly 16.
All inputs are finite; a program needn't handle non-finite values.
Results may differ from a plain program's by a relative error of at most 0.0061.
Values may be sent and summed in bfloat16 or wider, within the bound.
No kernel may reach another device: no remote copies, remote signals or barrier semaphores. Data moves between devices by JAX's collectives and lax.ppermute only.
A program may use at most 64 MiB of HBM per device.

v0:
```python
import jax
import jax.numpy as jnp
from jax import lax
from jax.sharding import PartitionSpec as P


def pull_rows(table, send_rows, valid):
    domains = lax.axis_size("dom")
    width = table.shape[1]
    picked = table[send_rows]
    picked = jnp.where(valid[:, None], picked, jnp.zeros_like(picked))
    moved = lax.all_to_all(
        picked.reshape(domains, -1, width), "dom", split_axis=0, concat_axis=0, tiled=True
    )
    return jnp.concatenate([table, moved.reshape(-1, width)], axis=0)


def push_rows(mirror_part, placement, own):
    domains = lax.axis_size("dom")
    width = own.shape[1]
    moved = lax.all_to_all(
        mirror_part.reshape(domains, -1, width), "dom", split_axis=0, concat_axis=0, tiled=True
    )
    return own + jnp.dot(placement, moved.reshape(-1, width), preferred_element_type=jnp.float32)


def edge_counts(sources, targets, relation, relations, local_rows):
    flat_index = (relation * local_rows + targets) * local_rows + sources
    ones = jnp.ones(sources.shape, jnp.float32)
    counted = jax.ops.segment_sum(
        ones, flat_index, num_segments=relations * local_rows * local_rows
    )
    return counted.reshape(relations, local_rows, local_rows).astype(jnp.bfloat16)


def per_device(
    master_rows,
    cotangent,
    relation_weight,
    self_weight,
    edge_source,
    edge_target,
    edge_relation,
    send_rows,
    send_counts,
):
    masters = master_rows[0]
    cotan = cotangent[0]
    sources = edge_source[0]
    targets = edge_target[0]
    relation = edge_relation[0]
    slots = send_rows[0]
    counts = send_counts[0]
    domains = lax.axis_size("dom")
    relations = relation_weight.shape[0]
    master_count = masters.shape[0]
    capacity = slots.shape[0] // domains
    valid = (jnp.arange(capacity)[None, :] < counts[:, None]).reshape(-1)
    placement = ((slots[None, :] == jnp.arange(master_count)[:, None]) & valid[None, :]).astype(
        jnp.bfloat16
    )
    table = pull_rows(masters, slots, valid)
    local_rows = table.shape[0]
    adjacency = edge_counts(sources, targets, relation, relations, local_rows)
    aggregated = jnp.einsum(
        "rij,jd->rid", adjacency, table, preferred_element_type=jnp.float32
    ).astype(jnp.bfloat16)
    partial_value = jnp.einsum(
        "rnd,rde->ne", aggregated, relation_weight, preferred_element_type=jnp.float32
    )
    own = partial_value[:master_count] + jnp.dot(
        masters, self_weight, preferred_element_type=jnp.float32
    )
    z_value = push_rows(partial_value[master_count:].astype(jnp.bfloat16), placement, own)
    activation = jax.nn.silu(z_value).astype(jnp.bfloat16)
    sigmoid_z = jax.nn.sigmoid(z_value)
    grad_z = (cotan.astype(jnp.float32) * sigmoid_z * (1.0 + z_value * (1.0 - sigmoid_z))).astype(
        jnp.bfloat16
    )
    grad_table = pull_rows(grad_z, slots, valid)
    relation_grad = jnp.einsum(
        "rnd,ne->rde", aggregated, grad_table, preferred_element_type=jnp.float32
    )
    self_grad = jnp.dot(masters.T, grad_z, preferred_element_type=jnp.float32)
    local_grads = jnp.concatenate([relation_grad, self_grad[None]], axis=0)
    group_part = lax.psum_scatter(local_grads, "grp", scatter_dimension=1, tiled=True)
    weight_grads = lax.psum(group_part, "dom")
    back = jnp.einsum(
        "rij,id->rjd", adjacency, grad_table, preferred_element_type=jnp.float32
    ).astype(jnp.bfloat16)
    back_partial = jnp.einsum(
        "rne,rde->nd", back, relation_weight, preferred_element_type=jnp.float32
    )
    back_own = back_partial[:master_count] + jnp.dot(
        grad_z, self_weight.T, preferred_element_type=jnp.float32
    )
    input_grad = push_rows(back_partial[master_count:].astype(jnp.bfloat16), placement, back_own)
    return (activation[None], input_grad.astype(jnp.bfloat16)[None], weight_grads)


def solution(mesh):
    return jax.shard_map(
        per_device,
        mesh=mesh,
        in_specs=(
            P("grp", "dom", None),
            P("grp", "dom", None),
            P(),
            P(),
            P("grp", "dom"),
            P("grp", "dom"),
            P("grp", "dom"),
            P("grp", "dom"),
            P("grp", "dom"),
        ),
        out_specs=(P("grp", "dom", None), P("grp", "dom", None), P(None, "grp", None)),
        check_vma=False,
    )
```

profile of v0, /device:TPU:0, one launch (start us, length us, event | category | flops | bytes accessed | tf_op | source)
XLA Modules:
  0.0 171.5 jit_solution(12031938624284277153)
XLA Ops:
  7.2 0.0 copy-start
  7.2 0.0 copy-start.1
  7.2 0.9 iota_compare_fusion.1
  8.1 0.7 fusion.23
  8.8 1.6 gather_fusion
  10.4 0.7 broadcast_select_fusion.1
  11.1 6.3 %all-to-all-start = ((bf16[4,16,512]{2,1,0:T(8,128)(2,1)}), bf16[4,16,512]{2,1,0:T(8,128)(2,1)}, u32[]{:S(2)}, u32[]{:S(2)}) async-start(bf16[4,16,512]{2,1,0:T(8,128)(2,1)} %broadcast_select_fusion.1), calls=%async_computation | async-start | bytes 131072 | tf_op jit(solution)/shard_map/all_to_all | solution.py:12
  17.4 0.7 multiply_add_fusion
  18.2 11.4 %scatter_custom_fusion = f32[147456]{0:T(1024)S(1)} fusion(s32[2048]{0:T(1024)S(1)} %bitcast.64, f32[2048]{0:T(1024)S(1)} %broadcast.65, f32[]{:T(128)} %constant.6.clone.1), kind=kCustom, calls=%fused_computation.16 | custom fusion | flops 2048 | bytes 589828 | tf_op jit(solution)/shard_map/scatter-add | solution.py:30
  29.6 0.3 convert_element_type.31
  29.9 0.0 all-to-all-done
  29.9 0.0 copy-done.1
  29.9 1.2 convolution_convert_fusion.1
  31.1 0.0 copy-done
  31.2 0.0 copy-start.5
  31.2 0.6 convolution_bitcast_fusion.1
  31.7 0.0 copy-start.3
  31.8 0.7 copy-done.3
  32.5 0.6 slice.31
  33.1 5.1 %all-to-all-start.1 = ((bf16[4,16,512]{2,1,0:T(8,128)(2,1)}), bf16[4,16,512]{2,1,0:T(8,128)(2,1)S(1)}, u32[]{:S(2)}, u32[]{:S(2)}) async-start(bf16[4,16,512]{2,1,0:T(8,128)(2,1)} %bitcast.10), calls=%async_computation.1 | async-start | bytes 131072 | tf_op jit(solution)/shard_map/all_to_all | solution.py:21
  38.2 0.1 lt.42
  38.3 5.7 %all-to-all-done.1 = bf16[4,16,512]{2,1,0:T(8,128)(2,1)S(1)} async-done(((bf16[4,16,512]{2,1,0:T(8,128)(2,1)}), bf16[4,16,512]{2,1,0:T(8,128)(2,1)S(1)}, u32[]{:S(2)}, u32[]{:S(2)}) %all-to-all-start.1) | async-done | bytes 65568 | tf_op jit(solution)/shard_map/all_to_all | solution.py:21
  44.0 0.0 copy-done.5
  44.0 0.2 fusion.17
  44.1 2.2 %fusion.9 = (bf16[128,512]{1,0:T(8,128)(2,1)S(1)}, bf16[1,128,512]{2,1,0:T(8,128)(2,1)}) fusion(bf16[1,128,512]{2,1,0:T(8,128)(2,1)} %param.10, f32[128,512]{1,0:T(8,128)S(1)} %fusion.17, bf16[512,512]{1,0:T(8,128)(2,1)} %param.12, bf16[1,128,512]{2,1,0:T(8,128)(2,1)S(1)} %copy-done.1, f32[192,512]{1,0:T(8,128)} %copy-done.3), kind=kOutput, calls=%fused_computation.20 | convolution fusion | flops 68026368 | bytes 1572864 | tf_op jit(solution)/shard_map/dot_general | solution.py:71
  46.3 1.3 gather_fusion.1
  47.6 1.5 broadcast_select_fusion
  49.2 3.9 %all-to-all-start.2 = ((bf16[4,16,512]{2,1,0:T(8,128)(2,1)}), bf16[4,16,512]{2,1,0:T(8,128)(2,1)}, u32[]{:S(2)}, u32[]{:S(2)}) async-start(bf16[4,16,512]{2,1,0:T(8,128)(2,1)} %broadcast_select_fusion), calls=%async_computation.2 | async-start | bytes 131072 | tf_op jit(solution)/shard_map/all_to_all | solution.py:12
  53.1 0.0 reduce-scatter.2.cloned.1.call-start
  53.1 1.3 convolution_bitcast_fusion
  54.5 4.4 %all-to-all-done.2 = bf16[4,16,512]{2,1,0:T(8,128)(2,1)} async-done(((bf16[4,16,512]{2,1,0:T(8,128)(2,1)}), bf16[4,16,512]{2,1,0:T(8,128)(2,1)}, u32[]{:S(2)}, u32[]{:S(2)}) %all-to-all-start.2) | async-done | bytes 65568 | tf_op jit(solution)/shard_map/all_to_all | solution.py:12
  58.9 0.0 copy-start.2
  58.9 1.7 fusion.13
  60.6 0.0 copy-done.2
  60.6 2.9 %pad_maximum_fusion = f32[5,512,512]{2,1,0:T(8,128)} fusion(f32[1,512,512]{2,1,0:T(8,128)S(1)} %copy-done.2, f32[4,512,512]{2,1,0:T(8,128)S(1)} %fusion.13), kind=kLoop, calls=%fused_computation.3 | loop fusion | flops 1310720 | bytes 10485760 | tf_op jit(solution)/shard_map/concatenate | solution.py:85
  63.5 0.0 reduce-scatter.2.cloned.1.call-update
  63.5 0.0 all-reduce.2.cloned.1.call-start
  63.5 55.1 %reduce-scatter.2.cloned.1.call-done = f32[5,64,512]{2,1,0:T(8,128)} async-done(((f32[5,512,512]{2,1,0:T(8,128)}), f32[5,64,512]{2,1,0:T(8,128)}) %reduce-scatter.2.cloned.1.call-update) | async-done | bytes 655376 | tf_op jit(solution)/shard_map/reduce_scatter | solution.py:86
  118.6 0.0 all-reduce.2.cloned.1.call-update
  118.7 0.0 copy-start.4
  118.7 2.7 %fusion.1 = f32[192,512]{1,0:T(8,128)} fusion(bf16[4,512,512]{2,1,0:T(8,128)(2,1)S(1)} %copy-done, bf16[4,192,192]{2,1,0:T(8,128)(2,1)S(1)} %convert_element_type.31, bf16[64,512]{1,0:T(8,128)(2,1)} %bitcast.15, bf16[128,512]{1,0:T(8,128)(2,1)S(1)} %get-tuple-element.3), kind=kOutput, calls=%fused_computation.8 | convolution fusion | flops 554434560 | bytes 2981888 | tf_op jit(solution)/shard_map/rne,rde->nd/dot_general | solution.py:91
  121.4 0.9 slice.30
  122.3 11.1 %all_to_all.20 = bf16[4,16,512]{2,1,0:T(8,128)(2,1)S(1)} all-to-all(bf16[4,16,512]{2,1,0:T(8,128)(2,1)S(1)} %bitcast.61), channel_id=1, replica_groups=mesh['dom'=4,'grp'=8] {'dom'}, dimensions={0} | all-to-all | bytes 131072 | tf_op jit(solution)/shard_map/all_to_all | solution.py:21
  133.4 0.2 fusion.15
  133.5 0.0 copy-done.4
  133.6 1.9 %fusion.5 = bf16[1,128,512]{2,1,0:T(8,128)(2,1)} fusion(f32[128,512]{1,0:T(8,128)S(1)} %fusion.15, bf16[128,512]{1,0:T(8,128)(2,1)S(1)} %get-tuple-element.3, bf16[512,512]{1,0:T(8,128)(2,1)S(1)} %copy-done.4, f32[192,512]{1,0:T(8,128)} %fusion.1), kind=kOutput, calls=%fused_computation.15 | convolution fusion | flops 67305472 | bytes 1310720 | tf_op jit(solution)/shard_map/dot_general | solution.py:94
  135.5 27.2 %all-reduce.2.cloned.1.call-done = f32[5,64,512]{2,1,0:T(8,128)} async-done(((f32[5,64,512]{2,1,0:T(8,128)}), f32[5,64,512]{2,1,0:T(8,128)}) %all-reduce.2.cloned.1.call-update) | async-done | bytes 655376 | tf_op jit(solution)/shard_map/psum | solution.py:87
  162.7 2.0 %copy.15 = f32[5,64,512]{2,1,0:T(8,128)} copy(f32[5,64,512]{2,1,0:T(8,128)} %all-reduce.2.cloned.1.call-done) | data formatting | bytes 1310720
  (3 shorter events, 0.0 us)
Async XLA Ops:
  7.2 24.0 %copy-start = (bf16[4,512,512]{2,1,0:T(8,128)(2,1)S(1)}, bf16[4,512,512]{2,1,0:T(8,128)(2,1)}, u32[]{:S(2)}) copy-start(bf16[4,512,512]{2,1,0:T(8,128)(2,1)} %param.11) | copy-start | bytes 6291460
  7.2 22.8 %copy-start.1 = (bf16[1,128,512]{2,1,0:T(8,128)(2,1)S(1)}, bf16[1,128,512]{2,1,0:T(8,128)(2,1)}, u32[]{:S(2)}) copy-start(bf16[1,128,512]{2,1,0:T(8,128)(2,1)} %param.9) | copy-start | bytes 393220
  11.1 18.8 %all-to-all-start = ((bf16[4,16,512]{2,1,0:T(8,128)(2,1)}), bf16[4,16,512]{2,1,0:T(8,128)(2,1)}, u32[]{:S(2)}, u32[]{:S(2)}) async-start(bf16[4,16,512]{2,1,0:T(8,128)(2,1)} %broadcast_select_fusion.1), calls=%async_computation | async-start | bytes 131072 | tf_op jit(solution)/shard_map/all_to_all | solution.py:12
  31.2 12.8 %copy-start.5 = (s32[1,64]{1,0:T(1,128)S(1)}, s32[1,64]{1,0:T(1,128)}, u32[]{:S(2)}) copy-start(s32[1,64]{1,0:T(1,128)} %param.16) | copy-start | bytes 772
  31.7 0.7 copy-start.3
  33.1 10.8 %all-to-all-start.1 = ((bf16[4,16,512]{2,1,0:T(8,128)(2,1)}), bf16[4,16,512]{2,1,0:T(8,128)(2,1)S(1)}, u32[]{:S(2)}, u32[]{:S(2)}) async-start(bf16[4,16,512]{2,1,0:T(8,128)(2,1)} %bitcast.10), calls=%async_computation.1 | async-start | bytes 131072 | tf_op jit(solution)/shard_map/all_to_all | solution.py:21
  49.2 9.7 %all-to-all-start.2 = ((bf16[4,16,512]{2,1,0:T(8,128)(2,1)}), bf16[4,16,512]{2,1,0:T(8,128)(2,1)}, u32[]{:S(2)}, u32[]{:S(2)}) async-start(bf16[4,16,512]{2,1,0:T(8,128)(2,1)} %broadcast_select_fusion), calls=%async_computation.2 | async-start | bytes 131072 | tf_op jit(solution)/shard_map/all_to_all | solution.py:12
  53.1 65.5 %reduce-scatter.2.cloned.1.call-start = ((), (), s32[]{:S(2)}) async-start(), calls=%async_computation.5 | async-start | bytes 5898240 | tf_op jit(solution)/shard_map/reduce_scatter | solution.py:86
  58.9 1.7 copy-start.2
  63.5 99.2 %all-reduce.2.cloned.1.call-start = ((), (), s32[]{:S(2)}) async-start(), calls=%async_computation.6 | async-start | bytes 1310720 | tf_op jit(solution)/shard_map/psum | solution.py:87
  118.7 14.9 %copy-start.4 = (bf16[512,512]{1,0:T(8,128)(2,1)S(1)}, bf16[512,512]{1,0:T(8,128)(2,1)}, u32[]{:S(2)}) copy-start(bf16[512,512]{1,0:T(8,128)(2,1)} %param.12) | copy-start | bytes 1572868
Sparse Core Ops, SparseCore 0:
  63.6 54.9 reduce-scatter.1
  121.0 41.6 all-reduce.1
where the time goes:
time: 172 us; the launch traced here: 171 us
  waiting for transfers between devices  92.4 us (54%)
  other arithmetic  18.9 us (11%)
  starting transfers between devices  15.4 us (9%)
  between operations  14.2 us (8%)
  matrix products  11.9 us (7%)
  blocking collectives  11.1 us (6%)
  local copies, waits for them, and re-layouts  7.62 us (4%)
    reduce_scatter x1, waiting for transfers between devices, per_device(): lax.psum_scatter(local_grads, 'grp', scatter_dimension=1, tiled=True)  55.1 us
    psum x1, waiting for transfers between devices, per_device(): weight_grads = lax.psum(group_part, 'dom')  27.2 us
    scatter-add x1, other arithmetic, edge_counts(): jax.ops.segment_sum(ones, flat_index, num_segments=relations * local_rows...  11.4 us
    all_to_all x1, blocking collectives, push_rows(): lax.all_to_all(mirror_part.reshape(domains, -1, width), 'dom', split_axis...  11.1 us
    all_to_all x2, starting transfers between devices, pull_rows(): lax.all_to_all(picked.reshape(domains, -1, width), 'dom', split_axis=0, c...  10.2 us
    all_to_all x1, waiting for transfers between devices, push_rows(): lax.all_to_all(mirror_part.reshape(domains, -1, width), 'dom', split_axis...  5.66 us
    all_to_all x1, starting transfers between devices, push_rows(): lax.all_to_all(mirror_part.reshape(domains, -1, width), 'dom', split_axis...  5.08 us
    all_to_all x2, waiting for transfers between devices, pull_rows(): lax.all_to_all(picked.reshape(domains, -1, width), 'dom', split_axis=0, c...  4.44 us
  transfers between devices with their start and end apart: 5, of which 4 were waited for; matrix products, arithmetic and copies ran while one was open for 11% of the time, Pallas kernels for 0%

commit v1 on v0

--- a/solution.py
+++ b/solution.py
@@ -84,7 +84,8 @@
     self_grad = jnp.dot(masters.T, grad_z, preferred_element_type=jnp.float32)
     local_grads = jnp.concatenate([relation_grad, self_grad[None]], axis=0)
     group_part = lax.psum_scatter(local_grads, "grp", scatter_dimension=1, tiled=True)
-    weight_grads = lax.psum(group_part, "dom")
+    blocks = lax.all_gather(group_part, "dom")
+    weight_grads = jnp.sum(blocks, axis=0)
     back = jnp.einsum(
         "rij,id->rjd", adjacency, grad_table, preferred_element_type=jnp.float32
     ).astype(jnp.bfloat16)

time: 172 us -> 186 us (1.081)
  waiting for transfers between devices: 92.4 us -> 106 us
  other arithmetic: 18.9 us -> 21.8 us
  local copies, waits for them, and re-layouts: 7.62 us -> 5.64 us
    all_gather x0 -> x1, waiting for transfers between devices: none -> 40.7 us  [per_device(): blocks = lax.all_gather(group_part, 'dom')]
    psum x1 -> x0, waiting for transfers between devices: 27.2 us -> none  [per_device(): weight_grads = lax.psum(group_part, 'dom')]
    reduce_sum x0 -> x1, other arithmetic: none -> 2.93 us  [per_device(): weight_grads = jnp.sum(blocks, axis=0)]
    unnamed x13 -> x12, local copies, waits for them, and re-layouts: 2.76 us -> 0.77 us
where the time goes in v1:
time: 186 us; the launch traced here: 185 us
  waiting for transfers between devices  106 us (57%)
  other arithmetic  21.8 us (12%)
  starting transfers between devices  15.4 us (8%)
  between operations  14.2 us (8%)
  matrix products  11.8 us (6%)
  blocking collectives  10.2 us (5%)
  local copies, waits for them, and re-layouts  5.64 us (3%)
    reduce_scatter x1, waiting for transfers between devices, per_device(): lax.psum_scatter(local_grads, 'grp', scatter_dimension=1, tiled=True)  55.1 us
    all_gather x1, waiting for transfers between devices, per_device(): blocks = lax.all_gather(group_part, 'dom')  40.7 us
    scatter-add x1, other arithmetic, edge_counts(): jax.ops.segment_sum(ones, flat_index, num_segments=relations * local_rows...  11.4 us
    all_to_all x2, starting transfers between devices, pull_rows(): lax.all_to_all(picked.reshape(domains, -1, width), 'dom', split_axis=0, c...  10.2 us
    all_to_all x1, blocking collectives, push_rows(): lax.all_to_all(mirror_part.reshape(domains, -1, width), 'dom', split_axis...  10.2 us
    all_to_all x1, waiting for transfers between devices, push_rows(): lax.all_to_all(mirror_part.reshape(domains, -1, width), 'dom', split_axis...  5.66 us
    all_to_all x1, starting transfers between devices, push_rows(): lax.all_to_all(mirror_part.reshape(domains, -1, width), 'dom', split_axis...  5.09 us
    all_to_all x2, waiting for transfers between devices, pull_rows(): lax.all_to_all(picked.reshape(domains, -1, width), 'dom', split_axis=0, c...  4.44 us
  transfers between devices with their start and end apart: 5, of which 4 were waited for; matrix products, arithmetic and copies ran while one was open for 11% of the time, Pallas kernels for 0%

profile of v1, /device:TPU:0, one launch (start us, length us, event | category | flops | bytes accessed | tf_op | source)
XLA Modules:
  0.0 185.1 jit_solution(16081815441345546200)
XLA Ops:
  7.2 0.0 copy-start
  7.2 0.0 copy-start.1
  7.2 0.9 iota_compare_fusion.1
  8.1 0.7 fusion.23
  8.8 1.6 gather_fusion
  10.4 0.7 broadcast_select_fusion.1
  11.1 6.3 %all-to-all-start = ((bf16[4,16,512]{2,1,0:T(8,128)(2,1)}), bf16[4,16,512]{2,1,0:T(8,128)(2,1)}, u32[]{:S(2)}, u32[]{:S(2)}) async-start(bf16[4,16,512]{2,1,0:T(8,128)(2,1)} %broadcast_select_fusion.1), calls=%async_computation | async-start | bytes 131072 | tf_op jit(solution)/shard_map/all_to_all | solution.py:12
  17.4 0.7 multiply_add_fusion
  18.2 11.4 %scatter_custom_fusion = f32[147456]{0:T(1024)S(1)} fusion(s32[2048]{0:T(1024)S(1)} %bitcast.66, f32[2048]{0:T(1024)S(1)} %broadcast.65, f32[]{:T(128)} %constant.6.clone.1), kind=kCustom, calls=%fused_computation.16 | custom fusion | flops 2048 | bytes 589828 | tf_op jit(solution)/shard_map/scatter-add | solution.py:30
  29.6 0.3 convert_element_type.31
  29.9 0.0 all-to-all-done
  29.9 0.0 copy-done.1
  29.9 1.2 convolution_convert_fusion.1
  31.1 0.0 copy-done
  31.1 0.0 copy-start.5
  31.2 0.6 convolution_bitcast_fusion.1
  31.7 0.0 copy-start.3
  31.7 0.7 copy-done.3
  32.5 0.6 slice.31
  33.1 5.1 %all-to-all-start.1 = ((bf16[4,16,512]{2,1,0:T(8,128)(2,1)}), bf16[4,16,512]{2,1,0:T(8,128)(2,1)S(1)}, u32[]{:S(2)}, u32[]{:S(2)}) async-start(bf16[4,16,512]{2,1,0:T(8,128)(2,1)} %bitcast.10), calls=%async_computation.1 | async-start | bytes 131072 | tf_op jit(solution)/shard_map/all_to_all | solution.py:21
  38.2 0.1 lt.42
  38.3 5.7 %all-to-all-done.1 = bf16[4,16,512]{2,1,0:T(8,128)(2,1)S(1)} async-done(((bf16[4,16,512]{2,1,0:T(8,128)(2,1)}), bf16[4,16,512]{2,1,0:T(8,128)(2,1)S(1)}, u32[]{:S(2)}, u32[]{:S(2)}) %all-to-all-start.1) | async-done | bytes 65568 | tf_op jit(solution)/shard_map/all_to_all | solution.py:21
  44.0 0.0 copy-done.5
  44.0 0.2 fusion.17
  44.1 2.2 %fusion.9 = (bf16[128,512]{1,0:T(8,128)(2,1)S(1)}, bf16[1,128,512]{2,1,0:T(8,128)(2,1)}) fusion(bf16[1,128,512]{2,1,0:T(8,128)(2,1)} %param.10, f32[128,512]{1,0:T(8,128)S(1)} %fusion.17, bf16[512,512]{1,0:T(8,128)(2,1)} %param.12, bf16[1,128,512]{2,1,0:T(8,128)(2,1)S(1)} %copy-done.1, f32[192,512]{1,0:T(8,128)} %copy-done.3), kind=kOutput, calls=%fused_computation.20 | convolution fusion | flops 68026368 | bytes 1572864 | tf_op jit(solution)/shard_map/dot_general | solution.py:71
  46.3 1.3 gather_fusion.1
  47.6 1.5 broadcast_select_fusion
  49.2 3.9 %all-to-all-start.2 = ((bf16[4,16,512]{2,1,0:T(8,128)(2,1)}), bf16[4,16,512]{2,1,0:T(8,128)(2,1)}, u32[]{:S(2)}, u32[]{:S(2)}) async-start(bf16[4,16,512]{2,1,0:T(8,128)(2,1)} %broadcast_select_fusion), calls=%async_computation.2 | async-start | bytes 131072 | tf_op jit(solution)/shard_map/all_to_all | solution.py:12
  53.1 0.0 reduce-scatter.2.cloned.1.call-start
  53.1 1.3 convolution_bitcast_fusion
  54.5 4.4 %all-to-all-done.2 = bf16[4,16,512]{2,1,0:T(8,128)(2,1)} async-done(((bf16[4,16,512]{2,1,0:T(8,128)(2,1)}), bf16[4,16,512]{2,1,0:T(8,128)(2,1)}, u32[]{:S(2)}, u32[]{:S(2)}) %all-to-all-start.2) | async-done | bytes 65568 | tf_op jit(solution)/shard_map/all_to_all | solution.py:12
  58.9 0.0 copy-start.2
  58.9 1.7 fusion.13
  60.6 0.0 copy-done.2
  60.6 2.9 %pad_maximum_fusion = f32[5,512,512]{2,1,0:T(8,128)} fusion(f32[1,512,512]{2,1,0:T(8,128)S(1)} %copy-done.2, f32[4,512,512]{2,1,0:T(8,128)S(1)} %fusion.13), kind=kLoop, calls=%fused_computation.3 | loop fusion | flops 1310720 | bytes 10485760 | tf_op jit(solution)/shard_map/concatenate | solution.py:85
  63.5 0.0 reduce-scatter.2.cloned.1.call-update
  63.5 0.0 all-gather.3.cloned.1.call-start
  63.5 55.1 %reduce-scatter.2.cloned.1.call-done = f32[5,64,512]{2,1,0:T(8,128)} async-done(((f32[5,512,512]{2,1,0:T(8,128)}), f32[5,64,512]{2,1,0:T(8,128)}) %reduce-scatter.2.cloned.1.call-update) | async-done | bytes 655376 | tf_op jit(solution)/shard_map/reduce_scatter | solution.py:86
  118.6 0.0 all-gather.3.cloned.1.call-update
  118.7 0.0 copy-start.4
  118.7 2.7 %fusion.1 = f32[192,512]{1,0:T(8,128)} fusion(bf16[4,512,512]{2,1,0:T(8,128)(2,1)S(1)} %copy-done, bf16[4,192,192]{2,1,0:T(8,128)(2,1)S(1)} %convert_element_type.31, bf16[64,512]{1,0:T(8,128)(2,1)} %bitcast.15, bf16[128,512]{1,0:T(8,128)(2,1)S(1)} %get-tuple-element.3), kind=kOutput, calls=%fused_computation.8 | convolution fusion | flops 554434560 | bytes 2981888 | tf_op jit(solution)/shard_map/rne,rde->nd/dot_general | solution.py:92
  121.4 0.9 slice.30
  122.3 10.2 %all_to_all.20 = bf16[4,16,512]{2,1,0:T(8,128)(2,1)S(1)} all-to-all(bf16[4,16,512]{2,1,0:T(8,128)(2,1)S(1)} %bitcast.63), channel_id=1, replica_groups=mesh['dom'=4,'grp'=8] {'dom'}, dimensions={0} | all-to-all | bytes 131072 | tf_op jit(solution)/shard_map/all_to_all | solution.py:21
  132.5 0.2 fusion.15
  132.7 0.0 copy-done.4
  132.7 1.9 %fusion.5 = bf16[1,128,512]{2,1,0:T(8,128)(2,1)} fusion(f32[128,512]{1,0:T(8,128)S(1)} %fusion.15, bf16[128,512]{1,0:T(8,128)(2,1)S(1)} %get-tuple-element.3, bf16[512,512]{1,0:T(8,128)(2,1)S(1)} %copy-done.4, f32[192,512]{1,0:T(8,128)} %fusion.1), kind=kOutput, calls=%fused_computation.15 | convolution fusion | flops 67305472 | bytes 1310720 | tf_op jit(solution)/shard_map/dot_general | solution.py:95
  134.6 40.7 %all-gather.3.cloned.1.call-done = f32[20,64,512]{2,1,0:T(8,128)} async-done(((f32[5,64,512]{2,1,0:T(8,128)}), f32[20,64,512]{2,1,0:T(8,128)}) %all-gather.3.cloned.1.call-update) | async-done | bytes 2621456 | tf_op jit(solution)/shard_map/all_gather | solution.py:87
  175.3 2.9 %reduce_sum.9 = f32[5,64,512]{2,1,0:T(8,128)} reduce(f32[4,5,64,512]{3,2,1,0:T(8,128)} %bitcast.60, f32[]{:T(128)} %constant.6.clone.1), dimensions={0}, to_apply=%region_2.3 | reduce | flops 491520 | bytes 3276804 | tf_op jit(solution)/shard_map/reduce_sum | solution.py:88
  (3 shorter events, 0.0 us)
Async XLA Ops:
  7.2 24.0 %copy-start = (bf16[4,512,512]{2,1,0:T(8,128)(2,1)S(1)}, bf16[4,512,512]{2,1,0:T(8,128)(2,1)}, u32[]{:S(2)}) copy-start(bf16[4,512,512]{2,1,0:T(8,128)(2,1)} %param.11) | copy-start | bytes 6291460
  7.2 22.8 %copy-start.1 = (bf16[1,128,512]{2,1,0:T(8,128)(2,1)S(1)}, bf16[1,128,512]{2,1,0:T(8,128)(2,1)}, u32[]{:S(2)}) copy-start(bf16[1,128,512]{2,1,0:T(8,128)(2,1)} %param.9) | copy-start | bytes 393220
  11.1 18.8 %all-to-all-start = ((bf16[4,16,512]{2,1,0:T(8,128)(2,1)}), bf16[4,16,512]{2,1,0:T(8,128)(2,1)}, u32[]{:S(2)}, u32[]{:S(2)}) async-start(bf16[4,16,512]{2,1,0:T(8,128)(2,1)} %broadcast_select_fusion.1), calls=%async_computation | async-start | bytes 131072 | tf_op jit(solution)/shard_map/all_to_all | solution.py:12
  31.1 12.8 %copy-start.5 = (s32[1,64]{1,0:T(1,128)S(1)}, s32[1,64]{1,0:T(1,128)}, u32[]{:S(2)}) copy-start(s32[1,64]{1,0:T(1,128)} %param.16) | copy-start | bytes 772
  31.7 0.7 copy-start.3
  33.1 10.8 %all-to-all-start.1 = ((bf16[4,16,512]{2,1,0:T(8,128)(2,1)}), bf16[4,16,512]{2,1,0:T(8,128)(2,1)S(1)}, u32[]{:S(2)}, u32[]{:S(2)}) async-start(bf16[4,16,512]{2,1,0:T(8,128)(2,1)} %bitcast.10), calls=%async_computation.1 | async-start | bytes 131072 | tf_op jit(solution)/shard_map/all_to_all | solution.py:21
  49.2 9.7 %all-to-all-start.2 = ((bf16[4,16,512]{2,1,0:T(8,128)(2,1)}), bf16[4,16,512]{2,1,0:T(8,128)(2,1)}, u32[]{:S(2)}, u32[]{:S(2)}) async-start(bf16[4,16,512]{2,1,0:T(8,128)(2,1)} %broadcast_select_fusion), calls=%async_computation.2 | async-start | bytes 131072 | tf_op jit(solution)/shard_map/all_to_all | solution.py:12
  53.1 65.5 %reduce-scatter.2.cloned.1.call-start = ((), (), s32[]{:S(2)}) async-start(), calls=%async_computation.5 | async-start | bytes 5898240 | tf_op jit(solution)/shard_map/reduce_scatter | solution.py:86
  58.9 1.7 copy-start.2
  63.5 111.9 %all-gather.3.cloned.1.call-start = ((), (), s32[]{:S(2)}) async-start(), calls=%async_computation.6 | async-start | bytes 3276800 | tf_op jit(solution)/shard_map/all_gather | solution.py:87
  118.7 14.0 %copy-start.4 = (bf16[512,512]{1,0:T(8,128)(2,1)S(1)}, bf16[512,512]{1,0:T(8,128)(2,1)}, u32[]{:S(2)}) copy-start(bf16[512,512]{1,0:T(8,128)(2,1)} %param.12) | copy-start | bytes 1572868
Sparse Core Ops, SparseCore 0:
  63.6 54.9 reduce-scatter.1
  120.2 55.0 all-gather.2
